TPU v7x, 256 devices: a whole 4x4x8 slice. The times are simulated.
256 devices in a mesh: section: 8 (over x, core), ep: 32 (over y, z).
Axes of the slice: x: 4, y: 4, z: 8, core: 2. Of those that a mesh axis runs over, the one named last changes fastest.
Arguments:
- hidden_states: bfloat16 [1536, 6144], P('ep'), may hold values from -6 to 6
- route_experts: int32 [1536, 2], P('ep'), may hold values from 0 to 7, all different within a row; in each aligned block of 48 rows (0 to 47, 48 to 95, ...) at most 24 rows name the same one
- route_weights: float32 [1536, 2], P('ep'), may hold values from 0.05 to 1
- gate_weight: bfloat16 [32, 6144, 2048], P('ep', None, 'section'), may hold values from -0.078125 to 0.078125
- up_weight: bfloat16 [32, 6144, 2048], P('ep', None, 'section'), may hold values from -0.078125 to 0.078125
- down_weight: bfloat16 [32, 2048, 6144], P('ep', 'section'), may hold values from -0.0625 to 0.0625
Outputs:
- layer_out: bfloat16 [1536, 6144], P('ep', 'section')
Inputs may be any that keep to these rules, and one draw needn't show every extreme that they name: `route_experts`: each row names two different experts. Among the 48 rows of one ep index no expert is named by more than 24 rows, and in every draw some expert is named by exactly 24 rows of some ep index.
All inputs are finite; a program needn't handle non-finite values.
Results may differ from a plain program's by a relative error of at most 0.015.
Values may be sent and summed in bfloat16 or wider, within the bound.
A program may use at most 128 MiB of HBM per device.

v0:
```python
import jax
import jax.numpy as jnp
from jax import lax
from jax.sharding import PartitionSpec as P

EXPERTS = 8


def cut_along(x, dim, peers):
    before, after = (x.shape[:dim], x.shape[dim + 1 :])
    return jnp.moveaxis(x.reshape(*before, peers, -1, *after), dim, 0)


def sent_and_summed(x, axis, dim):
    peers = lax.axis_size(axis)
    parts = lax.all_to_all(cut_along(x, dim, peers), axis, 0, 0, tiled=True)
    return jnp.sum(parts.astype(jnp.float32), axis=0)


def expert_rows(incoming, gate_weight, up_weight, down_weight):
    sources, slot_count, features = incoming.shape
    stacked = incoming.reshape(sources * slot_count, features)
    gate_value = jnp.dot(stacked, gate_weight[0], preferred_element_type=jnp.float32)
    up_value = jnp.dot(stacked, up_weight[0], preferred_element_type=jnp.float32)
    hidden = (jax.nn.silu(gate_value) * up_value).astype(jnp.bfloat16)
    result = jnp.dot(hidden, down_weight[0], preferred_element_type=jnp.float32).astype(
        jnp.bfloat16
    )
    return result.reshape(sources, slot_count, features)


def on_device(hidden_states, route_experts, route_weights, gate_weight, up_weight, down_weight):
    ep_count = lax.axis_size("ep")
    section_count = lax.axis_size("section")
    tok_rows, features = hidden_states.shape
    members = ep_count // EXPERTS
    capacity = tok_rows // 2
    chosen = route_experts.reshape(-1)
    one_hot = (chosen[:, None] == jnp.arange(EXPERTS, dtype=jnp.int32)[None, :]).astype(jnp.int32)
    earlier = jnp.cumsum(one_hot, axis=0) - one_hot
    slot_index = jnp.sum(earlier * one_hot, axis=1)
    position = (chosen * capacity + slot_index).reshape(tok_rows, 2)
    columns = jnp.arange(EXPERTS * capacity, dtype=jnp.int32)
    matches = position[:, :, None] == columns[None, None, :]
    select = jnp.sum(matches.astype(jnp.int32), axis=1).astype(jnp.bfloat16)
    weighing = jnp.sum(matches.astype(jnp.float32) * route_weights[:, :, None], axis=1)
    packed = jnp.einsum(
        "tj,td->jd", select, hidden_states, preferred_element_type=jnp.float32
    ).astype(jnp.bfloat16)
    outgoing = jnp.repeat(packed.reshape(EXPERTS, capacity, features), members, axis=0)
    slot_share = capacity // section_count
    first_slot = lax.axis_index("section") * slot_share
    own_slots = lax.dynamic_slice_in_dim(outgoing, first_slot, slot_share, 1)
    arrived = lax.all_to_all(own_slots, "ep", split_axis=0, concat_axis=0, tiled=True)
    partials = expert_rows(
        lax.all_gather(arrived, "section", axis=1, tiled=True), gate_weight, up_weight, down_weight
    )
    summed = lax.psum_scatter(
        partials.astype(jnp.float32).astype(jnp.bfloat16),
        "section",
        scatter_dimension=1,
        tiled=True,
    ).astype(jnp.float32)
    returned = lax.all_to_all(
        summed.astype(jnp.bfloat16), "ep", split_axis=0, concat_axis=0, tiled=True
    ).astype(summed.dtype)
    merged = jnp.sum(returned.reshape(EXPERTS, members, slot_share, features), axis=1)
    weigh_part = lax.dynamic_slice_in_dim(
        weighing.reshape(tok_rows, EXPERTS, capacity), first_slot, slot_share, 2
    )
    contribution = jnp.dot(
        weigh_part.reshape(tok_rows, EXPERTS * slot_share),
        merged.reshape(EXPERTS * slot_share, features),
        preferred_element_type=jnp.float32,
    )
    layer_out = sent_and_summed(contribution.astype(jnp.bfloat16), "section", 1)
    return layer_out.astype(jnp.bfloat16)


def solution(mesh):
    return jax.shard_map(
        on_device,
        mesh=mesh,
        in_specs=(
            P("ep", None),
            P("ep", None),
            P("ep", None),
            P("ep", None, "section"),
            P("ep", None, "section"),
            P("ep", "section", None),
        ),
        out_specs=P("ep", "section"),
        check_vma=False,
    )
```

profile of v0, /device:TPU:1, one launch (start us, length us, event | category | flops | bytes accessed | tf_op | source)
XLA Modules:
  0.0 317.6 jit_solution(11855568616730549436)
XLA Ops:
  6.5 0.9 copy.60
  7.7 0.1 reduce_window_sum.11
  7.8 0.2 select_reduce_fusion.1
  8.0 0.1 reduce_sum.51
  8.2 0.7 multiply_add_fusion
  9.0 1.9 convolution_convert_fusion.1
  10.8 4.8 %broadcast_in_dim.2 = bf16[8,4,24,6144]{3,2,1,0:T(8,128)(2,1)} broadcast(bf16[8,24,6144]{2,1,0:T(8,128)(2,1)S(1)} %bitcast.41), dimensions={0,2,3} | broadcast | bytes 11796480 | tf_op jit(solution)/shard_map/broadcast_in_dim | solution.py:50
  15.6 4.0 %constant_dynamic-slice_fusion.1 = bf16[32,3,6144]{2,1,0:T(4,128)(2,1)S(1)} fusion(bf16[32,24,6144]{2,1,0:T(8,128)(2,1)} %bitcast.37, s32[]{:T(128)S(6)} %select_n.4), kind=kLoop, calls=%fused_computation.30 | loop fusion | bytes 2359300 | tf_op jit(solution)/shard_map/dynamic_slice | solution.py:53
  19.6 48.3 %all_to_all.15 = bf16[32,3,6144]{2,1,0:T(4,128)(2,1)S(1)} all-to-all(bf16[32,3,6144]{2,1,0:T(4,128)(2,1)S(1)} %constant_dynamic-slice_fusion.1), channel_id=1, replica_groups=mesh['section'=8,'ep'=32] {'ep'}, dimensions={0} | all-to-all | bytes 2359296 | tf_op jit(solution)/shard_map/all_to_all | solution.py:54
  67.9 1.9 copy.64
  69.8 0.2 reduce-scatter.2.cloned.1.call-start
  70.0 57.2 %all-gather.2.cloned.1.call-done = bf16[32,24,6144]{2,0,1:T(8,128)(2,1)} async-done(((bf16[32,3,6144]{2,0,1:T(8,128)(2,1)}), bf16[32,24,6144]{2,0,1:T(8,128)(2,1)}) %all-gather.2.cloned.1.call-update) | async-done | bytes 9437200 | tf_op jit(solution)/shard_map/all_gather | solution.py:56
  127.2 12.5 %copy.65 = bf16[32,24,6144]{2,1,0:T(8,128)(2,1)} copy(bf16[32,24,6144]{2,0,1:T(8,128)(2,1)} %all-gather.2.cloned.1.call-done) | data formatting | bytes 18874368 | tf_op jit(solution)/shard_map/all_gather | solution.py:56
  139.7 8.1 %fusion.4 = f32[768,256]{1,0:T(8,128)} fusion(bf16[768,6144]{1,0:T(8,128)(2,1)} %bitcast.38, bf16[1,6144,256]{2,1,0:T(8,128)(2,1)} %param.9), kind=kOutput, calls=%fused_computation.8 | convolution fusion | flops 2415919104 | bytes 13369344 | tf_op jit(solution)/shard_map/dot_general | solution.py:23
  147.7 19.4 %convolution_convert_fusion = bf16[768,6144]{1,0:T(8,128)(2,1)} fusion(bf16[1,256,6144]{2,1,0:T(8,128)(2,1)S(1)} %copy-done, bf16[768,6144]{1,0:T(8,128)(2,1)} %bitcast.39, bf16[1,6144,256]{2,1,0:T(8,128)(2,1)} %param.10, f32[768,256]{1,0:T(8,128)} %fusion.4), kind=kOutput, calls=%fused_computation | convolution fusion | flops 4837736448 | bytes 25952256 | tf_op jit(solution)/shard_map/dot_general | solution.py:26
  167.1 12.5 %copy.66 = bf16[32,24,6144]{2,0,1:T(8,128)(2,1)} copy(bf16[32,24,6144]{2,1,0:T(8,128)(2,1)} %bitcast.40) | data formatting | bytes 18874368 | tf_op jit(solution)/shard_map/reshape | solution.py:29
  179.7 59.5 %reduce-scatter.2.cloned.1.call-done = bf16[32,3,6144]{2,0,1:T(8,128)(2,1)} async-done(((bf16[32,24,6144]{2,0,1:T(8,128)(2,1)}), bf16[32,3,6144]{2,0,1:T(8,128)(2,1)}) %reduce-scatter.2.cloned.1.call-update) | async-done | bytes 1179664 | tf_op jit(solution)/shard_map/reduce_scatter | solution.py:58
  239.1 3.4 %copy.67 = bf16[32,3,6144]{2,1,0:T(4,128)(2,1)} copy(bf16[32,3,6144]{2,0,1:T(8,128)(2,1)} %reduce-scatter.2.cloned.1.call-done) | data formatting | bytes 2359296 | tf_op jit(solution)/shard_map/reduce_scatter | solution.py:58
  242.5 9.7 %all-to-all-start.1 = ((bf16[32,3,6144]{2,1,0:T(4,128)(2,1)}), bf16[32,3,6144]{2,1,0:T(4,128)(2,1)}, u32[]{:S(2)}, u32[]{:S(2)}) async-start(bf16[32,3,6144]{2,1,0:T(4,128)(2,1)} %copy.67), calls=%async_computation.2 | async-start | bytes 3145728 | tf_op jit(solution)/shard_map/all_to_all | solution.py:64
  252.5 36.7 %all-to-all-done.1 = bf16[32,3,6144]{2,1,0:T(4,128)(2,1)} async-done(((bf16[32,3,6144]{2,1,0:T(4,128)(2,1)}), bf16[32,3,6144]{2,1,0:T(4,128)(2,1)}, u32[]{:S(2)}, u32[]{:S(2)}) %all-to-all-start.1) | async-done | bytes 1179680 | tf_op jit(solution)/shard_map/all_to_all | solution.py:64
  289.2 2.4 convert_reduce_fusion
  291.5 0.4 fusion
  292.0 17.0 %all_to_all.16 = bf16[8,48,768]{2,1,0:T(8,128)(2,1)} all-to-all(bf16[8,48,768]{2,1,0:T(8,128)(2,1)S(1)} %bitcast.43), channel_id=1, replica_groups=mesh['section'=8,'ep'=32] {'section'}, dimensions={0} | all-to-all | bytes 1179648 | tf_op jit(solution)/shard_map/all_to_all | solution.py:16
  308.9 1.8 reduce_sum.55
  (17 shorter events, 0.7 us)
Async XLA Ops:
  6.5 141.2 %copy-start = (bf16[1,256,6144]{2,1,0:T(8,128)(2,1)S(1)}, bf16[1,256,6144]{2,1,0:T(8,128)(2,1)}, u32[]{:S(2)}) copy-start(bf16[1,256,6144]{2,1,0:T(8,128)(2,1)} %param.11) | copy-start | bytes 9437188
  6.5 120.6 %all-gather.2.cloned.1.call-start = ((), (), s32[]{:S(2)}) async-start(), calls=%async_computation.4 | async-start | bytes 10616832 | tf_op jit(solution)/shard_map/all_gather | solution.py:56
  69.8 169.3 %reduce-scatter.2.cloned.1.call-start = ((), (), s32[]{:S(2)}) async-start(), calls=%async_computation.5 | async-start | bytes 10616832 | tf_op jit(solution)/shard_map/reduce_scatter | solution.py:58
  179.6 72.6 %copy-start.2 = (f32[48,2]{0,1:T(2,128)S(1)}, f32[48,2]{0,1:T(2,128)}, u32[]{:S(2)}) copy-start(f32[48,2]{0,1:T(2,128)} %param.8) | copy-start | bytes 1156
  242.5 46.6 %all-to-all-start.1 = ((bf16[32,3,6144]{2,1,0:T(4,128)(2,1)}), bf16[32,3,6144]{2,1,0:T(4,128)(2,1)}, u32[]{:S(2)}, u32[]{:S(2)}) async-start(bf16[32,3,6144]{2,1,0:T(4,128)(2,1)} %copy.67), calls=%async_computation.2 | async-start | bytes 3145728 | tf_op jit(solution)/shard_map/all_to_all | solution.py:64
  252.2 58.5 %copy-start.1 = (bf16[1,256,6144]{2,1,0:T(8,128)(2,1)S(1)}, bf16[1,256,6144]{2,1,0:T(8,128)(2,1)}, u32[]{:S(2)}) copy-start(bf16[1,256,6144]{2,1,0:T(8,128)(2,1)} %param.11) | copy-start | bytes 9437188
Sparse Core Ops, SparseCore 0:
  69.9 57.2 all-gather.1
  179.8 59.3 reduce-scatter.1
where the time goes:
time: 318 us
  waiting for transfers between devices  153 us (48%)
  blocking collectives  65.3 us (21%)
  local copies, waits for them, and re-layouts  40.4 us (13%)
  matrix products  29.7 us (9%)
  between operations  13.5 us (4%)
  starting transfers between devices  9.91 us (3%)
  other arithmetic  5.43 us (2%)
    reduce_scatter x1, waiting for transfers between devices, on_device(): lax.psum_scatter(partials.astype(jnp.float32).astype(jnp.bfloat16), 'sect...  59.5 us
    all_gather x1, waiting for transfers between devices, on_device(): lax.all_gather(arrived, 'section', axis=1, tiled=True)  57.2 us
    all_to_all x1, blocking collectives, on_device(): lax.all_to_all(own_slots, 'ep', split_axis=0, concat_axis=0, tiled=True)  48.3 us
    all_to_all x1, waiting for transfers between devices, on_device(): lax.all_to_all(summed.astype(jnp.bfloat16), 'ep', split_axis=0, concat_ax...  36.7 us
    dot_general x1, matrix products, expert_rows(): jnp.dot(hidden, down_weight[0], preferred_element_type=jnp.float32)  19.4 us
    all_to_all x1, blocking collectives, sent_and_summed(): parts = lax.all_to_all(cut_along(x, dim, peers), axis, 0, 0, tiled=True)  17 us
    reshape x1, local copies, waits for them, and re-layouts, expert_rows(): return result.reshape(sources, slot_count, features)  12.5 us
    all_gather x1, local copies, waits for them, and re-layouts, on_device(): lax.all_gather(arrived, 'section', axis=1, tiled=True)  12.5 us
  transfers between devices with their start and end apart: 3, of which 3 were waited for; matrix products, arithmetic and copies ran while one was open for 0% of the time, Pallas kernels for 0%

commit v1 on v0

--- a/solution.py
+++ b/solution.py
@@ -52,8 +52,11 @@
     first_slot = lax.axis_index("section") * slot_share
     own_slots = lax.dynamic_slice_in_dim(outgoing, first_slot, slot_share, 1)
     arrived = lax.all_to_all(own_slots, "ep", split_axis=0, concat_axis=0, tiled=True)
+    process_arrays = lambda mine_x, bus_axis, pos_dim: jnp.concatenate(
+        lax.all_to_all(jnp.stack(lax.psum(1, bus_axis) * [mine_x]), bus_axis, 0, 0), axis=pos_dim
+    )
     partials = expert_rows(
-        lax.all_gather(arrived, "section", axis=1, tiled=True), gate_weight, up_weight, down_weight
+        process_arrays(arrived, "section", 1), gate_weight, up_weight, down_weight
     )
     summed = lax.psum_scatter(
         partials.astype(jnp.float32).astype(jnp.bfloat16),

time: 318 us -> 408 us (1.28)
  blocking collectives: 65.3 us -> 178 us
  waiting for transfers between devices: 153 us -> 92.7 us
  local copies, waits for them, and re-layouts: 40.4 us -> 78.4 us
    all_to_all x0 -> x1, blocking collectives: none -> 113 us  [on_device(): lax.all_to_all(jnp.stack(lax.psum(1, bus_axis) * [mine_x]), bus_axis, 0, 0)]
    all_gather x1 -> x0, waiting for transfers between devices: 57.2 us -> none  [on_device(): lax.all_gather(arrived, 'section', axis=1, tiled=True)]
    reshape x0 -> x1, local copies, waits for them, and re-layouts: none -> 26.7 us  [on_device(): jnp.concatenate(lax.all_to_all(jnp.stack(lax.psum(1, bus_axis) * [mine_x]...]
    another operation x0 -> x2, local copies, waits for them, and re-layouts: none -> 24.7 us  [the longest x1 23.5 us: expert_rows(): stacked = incoming.reshape(sources * slot_count, features)]
    all_gather x1 -> x0, local copies, waits for them, and re-layouts: 12.5 us -> none  [on_device(): lax.all_gather(arrived, 'section', axis=1, tiled=True)]
  transfers between devices with their start and end apart: 3 -> 2, of which waited for: 3 -> 2; matrix products, arithmetic and copies ran while one was open for 0% -> 0% of each run, Pallas kernels for 0% -> 0%
where the time goes in v1:
time: 408 us; the launch traced here: 407 us
  blocking collectives  178 us (44%)
  waiting for transfers between devices  92.7 us (23%)
  local copies, waits for them, and re-layouts  78.4 us (19%)
  matrix products  29.7 us (7%)
  between operations  13.5 us (3%)
  starting transfers between devices  9.68 us (2%)
  other arithmetic  5.43 us (1%)
    all_to_all x1, blocking collectives, on_device(): lax.all_to_all(jnp.stack(lax.psum(1, bus_axis) * [mine_x]), bus_axis, 0, 0)  113 us
    reduce_scatter x1, waiting for transfers between devices, on_device(): lax.psum_scatter(partials.astype(jnp.float32).astype(jnp.bfloat16), 'sect...  56 us
    all_to_all x1, blocking collectives, on_device(): lax.all_to_all(own_slots, 'ep', split_axis=0, concat_axis=0, tiled=True)  48.3 us
    all_to_all x1, waiting for transfers between devices, on_device(): lax.all_to_all(summed.astype(jnp.bfloat16), 'ep', split_axis=0, concat_ax...  36.7 us
    reshape x1, local copies, waits for them, and re-layouts, on_device(): jnp.concatenate(lax.all_to_all(jnp.stack(lax.psum(1, bus_axis) * [mine_x]...  26.7 us
    another operation x1, local copies, waits for them, and re-layouts, expert_rows(): stacked = incoming.reshape(sources * slot_count, features)  23.5 us
    dot_general x1, matrix products, expert_rows(): jnp.dot(hidden, down_weight[0], preferred_element_type=jnp.float32)  19.4 us
    all_to_all x1, blocking collectives, sent_and_summed(): parts = lax.all_to_all(cut_along(x, dim, peers), axis, 0, 0, tiled=True)  16.9 us
  transfers between devices with their start and end apart: 2, of which 2 were waited for; matrix products, arithmetic and copies ran while one was open for 0% of the time, Pallas kernels for 0%

profile of v1, /device:TPU:1, one launch (start us, length us, event | category | flops | bytes accessed | tf_op | source)
XLA Modules:
  0.0 407.2 jit_solution(217330912048742869)
XLA Ops:
  6.5 0.9 copy.50
  7.7 0.1 reduce_window_sum.11
  7.8 0.2 select_reduce_fusion.1
  8.2 0.7 multiply_add_fusion
  9.0 1.9 convolution_convert_fusion.1
  10.8 4.8 %broadcast_in_dim.2 = bf16[8,4,24,6144]{3,2,1,0:T(8,128)(2,1)} broadcast(bf16[8,24,6144]{2,1,0:T(8,128)(2,1)S(1)} %bitcast.40), dimensions={0,2,3} | broadcast | bytes 11796480 | tf_op jit(solution)/shard_map/broadcast_in_dim | solution.py:50
  15.6 4.0 constant_dynamic-slice_fusion.1
  19.6 48.3 %all_to_all.20 = bf16[32,3,6144]{2,1,0:T(4,128)(2,1)S(1)} all-to-all(bf16[32,3,6144]{2,1,0:T(4,128)(2,1)S(1)} %constant_dynamic-slice_fusion.1), channel_id=1, replica_groups=mesh['section'=8,'ep'=32] {'ep'}, dimensions={0} | all-to-all | bytes 2359296 | tf_op jit(solution)/shard_map/all_to_all | solution.py:54
  67.9 0.9 copy.54
  68.8 1.2 stack.2
  69.9 112.6 %all_to_all.21 = bf16[8,32,3,6144]{3,1,2,0:T(8,128)(2,1)S(1)} all-to-all(bf16[8,32,3,6144]{3,1,2,0:T(8,128)(2,1)S(1)} %stack.2), channel_id=1, replica_groups=mesh['section'=8,'ep'=32] {'section'}, dimensions={0} | all-to-all | bytes 18874368 | tf_op jit(solution)/shard_map/all_to_all | solution.py:56
  182.6 26.7 %copy.55 = bf16[32,8,3,6144]{3,2,1,0:T(4,128)(2,1)} copy(bf16[32,8,3,6144]{3,0,2,1:T(8,128)(2,1)S(1)} %bitcast.37) | data formatting | bytes 18874368 | tf_op jit(solution)/shard_map/reshape | solution.py:55
  209.3 23.5 %reshape_reshape.3 = bf16[768,6144]{1,0:T(8,128)(2,1)} reshape(bf16[32,8,3,6144]{3,2,1,0:T(4,128)(2,1)} %copy.55) | data formatting | bytes 18874368 | tf_op jit(solution)/shard_map/reshape;reshape | solution.py:22
  232.8 8.1 %fusion.4 = f32[768,256]{1,0:T(8,128)} fusion(bf16[768,6144]{1,0:T(8,128)(2,1)} %reshape_reshape.3, bf16[1,6144,256]{2,1,0:T(8,128)(2,1)} %param.9), kind=kOutput, calls=%fused_computation.8 | convolution fusion | flops 2415919104 | bytes 13369344 | tf_op jit(solution)/shard_map/dot_general | solution.py:23
  240.9 19.4 %convolution_convert_fusion = bf16[768,6144]{1,0:T(8,128)(2,1)} fusion(bf16[1,256,6144]{2,1,0:T(8,128)(2,1)S(1)} %copy-done, bf16[768,6144]{1,0:T(8,128)(2,1)} %reshape_reshape.3, bf16[1,6144,256]{2,1,0:T(8,128)(2,1)} %param.10, f32[768,256]{1,0:T(8,128)} %fusion.4), kind=kOutput, calls=%fused_computation | convolution fusion | flops 4837736448 | bytes 25952256 | tf_op jit(solution)/shard_map/dot_general | solution.py:26
  260.3 12.5 %copy.56 = bf16[32,24,6144]{2,0,1:T(8,128)(2,1)} copy(bf16[32,24,6144]{2,1,0:T(8,128)(2,1)} %bitcast.39) | data formatting | bytes 18874368 | tf_op jit(solution)/shard_map/reshape | solution.py:29
  272.8 56.0 %reduce-scatter.2.cloned.1.call-done = bf16[32,3,6144]{2,0,1:T(8,128)(2,1)} async-done(((bf16[32,24,6144]{2,0,1:T(8,128)(2,1)}), bf16[32,3,6144]{2,0,1:T(8,128)(2,1)}) %reduce-scatter.2.cloned.1.call-update) | async-done | bytes 1179664 | tf_op jit(solution)/shard_map/reduce_scatter | solution.py:61
  328.7 3.4 copy.57
  332.2 9.7 %all-to-all-start.2 = ((bf16[32,3,6144]{2,1,0:T(4,128)(2,1)}), bf16[32,3,6144]{2,1,0:T(4,128)(2,1)}, u32[]{:S(2)}, u32[]{:S(2)}) async-start(bf16[32,3,6144]{2,1,0:T(4,128)(2,1)} %copy.57), calls=%async_computation.3 | async-start | bytes 3145728 | tf_op jit(solution)/shard_map/all_to_all | solution.py:67
  342.1 36.7 %all-to-all-done.2 = bf16[32,3,6144]{2,1,0:T(4,128)(2,1)} async-done(((bf16[32,3,6144]{2,1,0:T(4,128)(2,1)}), bf16[32,3,6144]{2,1,0:T(4,128)(2,1)}, u32[]{:S(2)}, u32[]{:S(2)}) %all-to-all-start.2) | async-done | bytes 1179680 | tf_op jit(solution)/shard_map/all_to_all | solution.py:67
  378.8 2.4 convert_reduce_fusion
  381.2 0.4 fusion
  381.6 16.9 %all_to_all.22 = bf16[8,48,768]{2,1,0:T(8,128)(2,1)} all-to-all(bf16[8,48,768]{2,1,0:T(8,128)(2,1)S(1)} %bitcast.42), channel_id=1, replica_groups=mesh['section'=8,'ep'=32] {'section'}, dimensions={0} | all-to-all | bytes 1179648 | tf_op jit(solution)/shard_map/all_to_all | solution.py:16
  398.6 1.8 reduce_sum.55
  (15 shorter events, 0.8 us)
Async XLA Ops:
  6.5 234.3 %copy-start = (bf16[1,256,6144]{2,1,0:T(8,128)(2,1)S(1)}, bf16[1,256,6144]{2,1,0:T(8,128)(2,1)}, u32[]{:S(2)}) copy-start(bf16[1,256,6144]{2,1,0:T(8,128)(2,1)} %param.11) | copy-start | bytes 9437188
  6.5 322.2 %reduce-scatter.2.cloned.1.call-start = ((), (), s32[]{:S(2)}) async-start(), calls=%async_computation.5 | async-start | bytes 10616832 | tf_op jit(solution)/shard_map/reduce_scatter | solution.py:61
  272.8 69.1 %copy-start.1 = (f32[48,2]{0,1:T(2,128)S(1)}, f32[48,2]{0,1:T(2,128)}, u32[]{:S(2)}) copy-start(f32[48,2]{0,1:T(2,128)} %param.8) | copy-start | bytes 1156
  332.2 46.7 %all-to-all-start.2 = ((bf16[32,3,6144]{2,1,0:T(4,128)(2,1)}), bf16[32,3,6144]{2,1,0:T(4,128)(2,1)}, u32[]{:S(2)}, u32[]{:S(2)}) async-start(bf16[32,3,6144]{2,1,0:T(4,128)(2,1)} %copy.57), calls=%async_computation.3 | async-start | bytes 3145728 | tf_op jit(solution)/shard_map/all_to_all | solution.py:67
Sparse Core Ops, SparseCore 0:
  272.9 55.8 reduce-scatter.1
